TPU v7x, 32 devices: a whole 2x2x4 slice. The times are simulated.
32 devices in a mesh: dp: 8 (over z, y), row: 2 (over x), col: 2 (over core).
Axes of the slice: x: 2, y: 2, z: 4, core: 2. Of those that a mesh axis runs over, the one named last changes fastest.
Arguments:
- stream: bfloat16 [4096, 2560], P(('dp', 'row'), 'col'), may hold values from -45 to 45
- scale_first: float32 [2560], P('col'), may hold values from -0.5 to 0.5
- branch_weight: bfloat16 [2560, 2560], P('col', ('row', 'dp')), may hold values from -0.125 to 0.125
- branch_bias: float32 [2560], P('row'), may hold values from -3 to 3
- mixer_weight: bfloat16 [2560, 2560], P('col', ('row', 'dp')), may hold values from -0.125 to 0.125
- mixer_bias: float32 [2560], P('row'), may hold values from -3 to 3
- conv_weight: float32 [4, 2560], P(None, 'row'), may hold values from -3 to 3
- conv_bias: float32 [2560], P('row'), may hold values from -2 to 2
- decay_weight: bfloat16 [10, 256, 256], P('row'), may hold values from -0.375 to 0.375
- decay_bias: float32 [2560], P('row'), may hold values from -3 to 3
- input_weight: bfloat16 [10, 256, 256], P('row'), may hold values from -0.375 to 0.375
- input_bias: float32 [2560], P('row'), may hold values from -3 to 3
- decay_param: float32 [2560], P('row'), may hold values from -13 to -4
- output_weight: bfloat16 [2560, 2560], P('row', ('col', 'dp')), may hold values from -0.3125 to 0.3125
- output_bias: float32 [2560], P('col'), may hold values from -3 to 3
- scale_second: float32 [2560], P('col'), may hold values from -0.5 to 0.5
- gate_weight: bfloat16 [2560, 7680], P('col', ('row', 'dp')), may hold values from -0.125 to 0.125
- gate_bias: float32 [7680], P('row'), may hold values from -3 to 3
- up_weight: bfloat16 [2560, 7680], P('col', ('row', 'dp')), may hold values from -0.125 to 0.125
- up_bias: float32 [7680], P('row'), may hold values from -3 to 3
- down_weight: bfloat16 [7680, 2560], P('row', ('col', 'dp')), may hold values from -0.09375 to 0.09375
- down_bias: float32 [2560], P('col'), may hold values from -3 to 3
- cotangent: bfloat16 [4096, 2560], P(('dp', 'row'), 'col'), may hold values from -6 to 6
Outputs:
- result: bfloat16 [4096, 2560], P(('dp', 'row'), 'col')
- grad_stream: float32 [4096, 2560], P(('dp', 'row'), 'col')
- grad_scale_first: float32 [2560], P('col')
- grad_branch_weight: float32 [2560, 2560], P('col', ('row', 'dp'))
- grad_branch_bias: float32 [2560], P('row')
- grad_mixer_weight: float32 [2560, 2560], P('col', ('row', 'dp'))
- grad_mixer_bias: float32 [2560], P('row')
- grad_conv_weight: float32 [4, 2560], P(None, 'row')
- grad_conv_bias: float32 [2560], P('row')
- grad_decay_weight: float32 [10, 256, 256], P('row')
- grad_decay_bias: float32 [2560], P('row')
- grad_input_weight: float32 [10, 256, 256], P('row')
- grad_input_bias: float32 [2560], P('row')
- grad_decay_param: float32 [2560], P('row')
- grad_output_weight: float32 [2560, 2560], P('row', ('col', 'dp'))
- grad_output_bias: float32 [2560], P('col')
- grad_scale_second: float32 [2560], P('col')
- grad_gate_weight: float32 [2560, 7680], P('col', ('row', 'dp'))
- grad_gate_bias: float32 [7680], P('row')
- grad_up_weight: float32 [2560, 7680], P('col', ('row', 'dp'))
- grad_up_bias: float32 [7680], P('row')
- grad_down_weight: float32 [7680, 2560], P('row', ('col', 'dp'))
- grad_down_bias: float32 [2560], P('col')
All inputs are finite; a program needn't handle non-finite values.
Results may differ from a plain program's by a relative error of at most 0.022.
Values may be sent and summed in bfloat16 or wider, within the bound.
A program may use at most 320 MiB of HBM per device.

v0:
```python
import jax
import jax.numpy as jnp
from jax import lax
from jax.sharding import PartitionSpec as P

D = 2560
CONV = 4
LEN = 4096


EPSILON = 1e-06
SQRT_FLOOR = 0.0001
CONTRACT_LAST = (((1,), (1,)), ((), ()))
CONTRACT_FIRST = (((0,), (0,)), ((), ()))


def from_behind(x, axis, by):
    peers = lax.axis_size(axis)
    pairs = [(i, i + by) for i in range(peers) if 0 <= i + by < peers]
    return lax.ppermute(x, axis, pairs)


def prefix(value, axis, join, neutral, backward):
    count, mine = (lax.axis_size(axis), lax.axis_index(axis))
    pieces = jax.tree.map(lambda part: lax.all_gather(part, axis), value)
    if backward:
        pieces = jax.tree.map(lambda part: part[::-1], pieces)
        mine = count - 1 - mine
    running = jax.tree.map(
        lambda part, zero: jnp.full_like(part, 0) + jnp.asarray(zero, part.dtype), value, neutral
    )

    def lap(position, running):
        longer = join(running, jax.tree.map(lambda part: part[position], pieces))
        return jax.tree.map(lambda new, old: jnp.where(position < mine, new, old), longer, running)

    return lax.fori_loop(0, count - 1, lap, running)


def gelu_tanh(values):
    return jax.nn.gelu(values, approximate=True)


def gates_of(decay_pre, input_pre, decay_param, conv_low, starts):
    rate_gate = jax.nn.sigmoid(decay_pre)
    in_gate = jax.nn.sigmoid(input_pre)
    log_decay = -8.0 * jax.nn.softplus(decay_param) * rate_gate
    retain = jnp.where(starts, 0.0, jnp.exp(log_decay))
    multiplier = jnp.where(
        starts, 1.0, jnp.sqrt(jnp.maximum(-jnp.expm1(2.0 * log_decay), SQRT_FLOOR))
    )
    return (retain, multiplier * in_gate * conv_low)


def affine(earlier, latter):
    return (earlier[0] * latter[0], latter[0] * earlier[1] + latter[1])


def feature_total(values):
    return lax.psum(values, "col")


def normalize(values, scale_vec):
    inverse = lax.rsqrt(
        feature_total(jnp.sum(values * values, axis=1, keepdims=True)) / D + EPSILON
    )
    return (values * inverse * (1.0 + scale_vec), inverse)


def normalize_back(gradient, values, inverse, scale_vec):
    weighted = gradient * (1.0 + scale_vec)
    scale_grad = jnp.sum(gradient * values * inverse, axis=0)
    inner_sum = feature_total(jnp.sum(weighted * values, axis=1, keepdims=True))
    return (inverse * weighted - values * inverse**3 * inner_sum / D, scale_grad)


def rows_then_cols(local_part, product):
    gathered = lax.all_gather(local_part, "row", axis=0, tiled=True)
    return (gathered, lax.psum_scatter(product(gathered), "col", scatter_dimension=0, tiled=True))


def cols_then_rows(local_part, product):
    gathered = lax.all_gather(local_part, "col", axis=0, tiled=True)
    return (
        gathered,
        lax.psum_scatter(
            product(gathered).astype(jnp.bfloat16), "row", scatter_dimension=0, tiled=True
        ).astype(jnp.float32),
    )


def fetch_weights(branch_weight, mixer_weight, output_weight, gate_weight, up_weight, down_weight):
    gathered = (
        lax.all_gather(branch_weight, "dp", axis=1, tiled=True),
        lax.all_gather(mixer_weight, "dp", axis=1, tiled=True),
        lax.all_gather(output_weight, "dp", axis=1, tiled=True),
        lax.all_gather(gate_weight, "dp", axis=1, tiled=True),
        lax.all_gather(up_weight, "dp", axis=1, tiled=True),
        lax.all_gather(down_weight, "dp", axis=1, tiled=True),
    )
    first_pair = jnp.concatenate([gathered[0], gathered[1]], axis=1)
    second_pair = jnp.concatenate([gathered[3], gathered[4]], axis=1)
    return (first_pair, gathered[2], second_pair, gathered[5])


def sum_grads(first_grad, second_grad, third_grad):
    return (
        lax.psum_scatter(
            first_grad.astype(jnp.bfloat16), "dp", scatter_dimension=1, tiled=True
        ).astype(jnp.float32),
        lax.psum_scatter(
            second_grad.astype(jnp.bfloat16), "dp", scatter_dimension=1, tiled=True
        ).astype(jnp.float32),
        lax.psum_scatter(
            third_grad.astype(jnp.bfloat16), "dp", scatter_dimension=1, tiled=True
        ).astype(jnp.float32),
    )


def on_device(
    stream,
    scale_first,
    branch_weight,
    branch_bias,
    mixer_weight,
    mixer_bias,
    conv_weight,
    conv_bias,
    decay_weight,
    decay_bias,
    input_weight,
    input_bias,
    decay_param,
    output_weight,
    output_bias,
    scale_second,
    gate_weight,
    gate_bias,
    up_weight,
    up_bias,
    down_weight,
    down_bias,
    cotangent,
):
    first_pair, full_output, second_pair, full_down = fetch_weights(
        branch_weight, mixer_weight, output_weight, gate_weight, up_weight, down_weight
    )
    inner_width = first_pair.shape[1] // 2
    hidden_width = second_pair.shape[1] // 2
    stream_wide = stream.astype(jnp.float32)
    normed_first, inverse_first = normalize(stream_wide, scale_first)
    first_rows, first_proj = rows_then_cols(
        normed_first.astype(jnp.bfloat16),
        lambda pieces: jnp.dot(pieces, first_pair, preferred_element_type=jnp.float32),
    )
    branch_pre = first_proj[:, :inner_width] + branch_bias
    mixer_pre = first_proj[:, inner_width:] + mixer_bias
    branch_act, branch_back = jax.vjp(gelu_tanh, branch_pre)
    steps_here = mixer_pre.shape[0]
    first_token = lax.axis_index(("dp", "col")) * steps_here
    position = (first_token + jnp.arange(steps_here, dtype=jnp.int32)) % LEN
    margin = CONV - 1
    left_edge = from_behind(mixer_pre[steps_here - margin :], ("dp", "col"), 1)
    padded = jnp.concatenate([left_edge, mixer_pre], axis=0)
    conv_out = conv_bias + jnp.zeros_like(mixer_pre)
    for offset in range(CONV):
        in_reach = (position >= offset)[:, None]
        conv_out = conv_out + jnp.where(
            in_reach,
            conv_weight[offset] * padded[margin - offset : margin - offset + steps_here],
            0.0,
        )
    conv_low = conv_out.astype(jnp.bfloat16)
    conv_wide = conv_low.astype(jnp.float32)
    heads_here = decay_weight.shape[0]
    block_width = decay_weight.shape[1]
    conv_heads = conv_low.reshape(steps_here, heads_here, block_width)
    decay_pre = (
        jnp.einsum(
            "thi,hij->thj", conv_heads, decay_weight, preferred_element_type=jnp.float32
        ).reshape(steps_here, inner_width)
        + decay_bias
    )
    input_pre = (
        jnp.einsum(
            "thi,hij->thj", conv_heads, input_weight, preferred_element_type=jnp.float32
        ).reshape(steps_here, inner_width)
        + input_bias
    )
    starts = (position == 0)[:, None]

    def gate_values(decay_in, input_in, param_in, conv_in):
        return gates_of(decay_in, input_in, param_in, conv_in, starts)

    (retain, source), gate_back = jax.vjp(gate_values, decay_pre, input_pre, decay_param, conv_wide)
    cumulative, local_state = lax.associative_scan(affine, (retain, source), axis=0)
    ones_row = jnp.ones((inner_width,), jnp.float32)
    zero_row = jnp.zeros((inner_width,), jnp.float32)
    carry_decay, state_in = prefix(
        (cumulative[-1], local_state[-1]), ("dp", "col"), affine, (ones_row, zero_row), False
    )
    states = local_state + cumulative * state_in
    mixed_low = (states * branch_act).astype(jnp.bfloat16)
    mixed_rows, out_proj = cols_then_rows(
        mixed_low, lambda pieces: jnp.dot(pieces, full_output, preferred_element_type=jnp.float32)
    )
    first_out = stream_wide + out_proj + output_bias
    normed_second, inverse_second = normalize(first_out, scale_second)
    second_rows, second_proj = rows_then_cols(
        normed_second.astype(jnp.bfloat16),
        lambda pieces: jnp.dot(pieces, second_pair, preferred_element_type=jnp.float32),
    )
    gate_pre = second_proj[:, :hidden_width] + gate_bias
    up_pre = second_proj[:, hidden_width:] + up_bias
    hidden, hidden_back = jax.vjp(
        lambda gate_in, up_in: gelu_tanh(gate_in) * up_in, gate_pre, up_pre
    )
    hidden_rows, down_proj = cols_then_rows(
        hidden.astype(jnp.bfloat16),
        lambda pieces: jnp.dot(pieces, full_down, preferred_element_type=jnp.float32),
    )
    result = (first_out + down_proj + down_bias).astype(jnp.bfloat16)
    delta_result = cotangent.astype(jnp.float32)
    down_rows, delta_hidden = rows_then_cols(
        delta_result.astype(jnp.bfloat16),
        lambda pieces: lax.dot_general(
            pieces, full_down, CONTRACT_LAST, preferred_element_type=jnp.float32
        ),
    )
    grad_down = lax.dot_general(
        hidden_rows, down_rows, CONTRACT_FIRST, preferred_element_type=jnp.float32
    )
    delta_gate, delta_up = hidden_back(delta_hidden)
    pair_low = jnp.concatenate([delta_gate, delta_up], axis=1).astype(jnp.bfloat16)
    pair_rows, delta_normed_second = cols_then_rows(
        pair_low,
        lambda pieces: lax.dot_general(
            pieces, second_pair, CONTRACT_LAST, preferred_element_type=jnp.float32
        ),
    )
    grad_pair = lax.dot_general(
        second_rows, pair_rows, CONTRACT_FIRST, preferred_element_type=jnp.float32
    )
    grad_gate = grad_pair[:, :hidden_width]
    grad_up = grad_pair[:, hidden_width:]
    norm_second_part, grad_scale_second = normalize_back(
        delta_normed_second, first_out, inverse_second, scale_second
    )
    delta_first = delta_result + norm_second_part
    out_rows, delta_mixed = rows_then_cols(
        delta_first.astype(jnp.bfloat16),
        lambda pieces: lax.dot_general(
            pieces, full_output, CONTRACT_LAST, preferred_element_type=jnp.float32
        ),
    )
    grad_output = lax.dot_general(
        mixed_rows, out_rows, CONTRACT_FIRST, preferred_element_type=jnp.float32
    )
    delta_state = delta_mixed * branch_act
    (delta_branch,) = branch_back(delta_mixed * states)
    retain_next = jnp.concatenate([retain[1:], ones_row[None]], axis=0)
    suffix_rev, back_rev = lax.associative_scan(
        affine, (retain_next[::-1], delta_state[::-1]), axis=0
    )
    suffix = suffix_rev[::-1]
    local_back = back_rev[::-1]
    lead_retain = retain[0]
    carry_scale, back_in = prefix(
        (lead_retain * suffix[0], lead_retain * local_back[0]),
        ("dp", "col"),
        affine,
        (ones_row, zero_row),
        True,
    )
    back_state = local_back + suffix * back_in
    state_prev = jnp.concatenate([state_in[None], states[:-1]], axis=0)
    delta_decay_pre, delta_input_pre, grad_decay_param, delta_conv = gate_back(
        (back_state * state_prev, back_state)
    )
    decay_low = delta_decay_pre.astype(jnp.bfloat16).reshape(steps_here, heads_here, block_width)
    input_low = delta_input_pre.astype(jnp.bfloat16).reshape(steps_here, heads_here, block_width)
    grad_decay_weight = jnp.einsum(
        "thi,thj->hij", conv_heads, decay_low, preferred_element_type=jnp.float32
    )
    grad_input_weight = jnp.einsum(
        "thi,thj->hij", conv_heads, input_low, preferred_element_type=jnp.float32
    )
    delta_conv = delta_conv + jnp.einsum(
        "thj,hij->thi", decay_low, decay_weight, preferred_element_type=jnp.float32
    ).reshape(steps_here, inner_width)
    delta_conv = delta_conv + jnp.einsum(
        "thj,hij->thi", input_low, input_weight, preferred_element_type=jnp.float32
    ).reshape(steps_here, inner_width)
    delta_padded = jnp.zeros_like(padded)
    conv_grads = []
    for offset in range(CONV):
        in_reach = (position >= offset)[:, None]
        masked = jnp.where(in_reach, delta_conv, 0.0)
        conv_grads.append(
            jnp.sum(masked * padded[margin - offset : margin - offset + steps_here], axis=0)
        )
        delta_padded = delta_padded + jnp.pad(
            masked * conv_weight[offset], ((margin - offset, offset), (0, 0))
        )
    grad_conv_weight = jnp.stack(conv_grads, axis=0)
    right_edge = from_behind(delta_padded[:margin], ("dp", "col"), -1)
    delta_mixer = delta_padded[margin:] + jnp.pad(right_edge, ((steps_here - margin, 0), (0, 0)))
    first_low = jnp.concatenate([delta_branch, delta_mixer], axis=1).astype(jnp.bfloat16)
    back_rows, delta_normed_first = cols_then_rows(
        first_low,
        lambda pieces: lax.dot_general(
            pieces, first_pair, CONTRACT_LAST, preferred_element_type=jnp.float32
        ),
    )
    grad_first = lax.dot_general(
        first_rows, back_rows, CONTRACT_FIRST, preferred_element_type=jnp.float32
    )
    norm_first_part, grad_scale_first = normalize_back(
        delta_normed_first, stream_wide, inverse_first, scale_first
    )
    grad_stream = delta_first + norm_first_part
    summed_gate, summed_up, summed_down = sum_grads(grad_gate, grad_up, grad_down)
    summed_branch, summed_mixer, summed_output = sum_grads(
        grad_first[:, :inner_width], grad_first[:, inner_width:], grad_output
    )
    stream_sums = lax.psum(
        (
            grad_scale_first,
            grad_scale_second,
            jnp.sum(delta_first, axis=0),
            jnp.sum(delta_result, axis=0),
        ),
        ("dp", "row"),
    )
    inner_sums = lax.psum(
        (
            jnp.sum(delta_branch, axis=0),
            jnp.sum(delta_mixer, axis=0),
            grad_conv_weight,
            jnp.sum(delta_conv, axis=0),
            grad_decay_weight,
            jnp.sum(delta_decay_pre, axis=0),
            grad_input_weight,
            jnp.sum(delta_input_pre, axis=0),
            grad_decay_param,
            jnp.sum(delta_gate, axis=0),
            jnp.sum(delta_up, axis=0),
        ),
        ("dp", "col"),
    )
    return (
        result,
        grad_stream,
        stream_sums[0],
        summed_branch,
        inner_sums[0],
        summed_mixer,
        inner_sums[1],
        inner_sums[2],
        inner_sums[3],
        inner_sums[4],
        inner_sums[5],
        inner_sums[6],
        inner_sums[7],
        inner_sums[8],
        summed_output,
        stream_sums[2],
        stream_sums[1],
        summed_gate,
        inner_sums[9],
        summed_up,
        inner_sums[10],
        summed_down,
        stream_sums[3],
    )


def solution(mesh):
    return jax.shard_map(
        on_device,
        mesh=mesh,
        in_specs=(
            P(("dp", "row"), "col"),
            P("col"),
            P("col", ("row", "dp")),
            P("row"),
            P("col", ("row", "dp")),
            P("row"),
            P(None, "row"),
            P("row"),
            P("row", None, None),
            P("row"),
            P("row", None, None),
            P("row"),
            P("row"),
            P("row", ("col", "dp")),
            P("col"),
            P("col"),
            P("col", ("row", "dp")),
            P("row"),
            P("col", ("row", "dp")),
            P("row"),
            P("row", ("col", "dp")),
            P("col"),
            P(("dp", "row"), "col"),
        ),
        out_specs=(
            P(("dp", "row"), "col"),
            P(("dp", "row"), "col"),
            P("col"),
            P("col", ("row", "dp")),
            P("row"),
            P("col", ("row", "dp")),
            P("row"),
            P(None, "row"),
            P("row"),
            P("row", None, None),
            P("row"),
            P("row", None, None),
            P("row"),
            P("row"),
            P("row", ("col", "dp")),
            P("col"),
            P("col"),
            P("col", ("row", "dp")),
            P("row"),
            P("col", ("row", "dp")),
            P("row"),
            P("row", ("col", "dp")),
            P("col"),
        ),
        check_vma=False,
    )
```

profile of v0, /device:TPU:0, one launch (start us, length us, event | category | flops | bytes accessed | tf_op | source)
XLA Modules:
  0.0 2509.1 jit_solution(12616008123017626827)
XLA Ops:
  14.4 60.0 %all-gather.21.cloned.1.call-done = bf16[1280,1280]{0,1:T(8,128)(2,1)} async-done(((bf16[1280,160]{0,1:T(8,128)(2,1)}), bf16[1280,1280]{0,1:T(8,128)(2,1)}) %all-gather.21.cloned.1.call-update) | async-done | bytes 3276816 | tf_op jit(solution)/shard_map/all_gather | solution.py:94
  78.3 58.5 %all-gather.23.cloned.1.call-done = bf16[1280,1280]{0,1:T(8,128)(2,1)} async-done(((bf16[1280,160]{0,1:T(8,128)(2,1)}), bf16[1280,1280]{0,1:T(8,128)(2,1)}) %all-gather.23.cloned.1.call-update) | async-done | bytes 3276816 | tf_op jit(solution)/shard_map/all_gather | solution.py:95
  140.7 21.2 all-gather.19.cloned.1.call-done
  161.9 9.1 fusion.91
  171.9 12.3 reduce-scatter.23.cloned.1.call-done
  373.2 4.8 pad.249
  385.7 23.9 all-gather
  422.1 17.7 all-gather.1
  446.2 7.6 all-gather.25.cloned.1.call-done
  453.8 5.3 convolution_convert_fusion.7
  462.0 21.7 reduce-scatter.25.cloned.1.call-done
  489.9 19.6 all-gather.39.cloned.1.call-done
  509.5 144.5 %all-gather.37.cloned.1.call-done = bf16[3840,1280]{0,1:T(8,128)(2,1)} async-done(((bf16[3840,160]{0,1:T(8,128)(2,1)}), bf16[3840,1280]{0,1:T(8,128)(2,1)}) %all-gather.37.cloned.1.call-update) | async-done | bytes 9830416 | tf_op jit(solution)/shard_map/all_gather | solution.py:99
  654.0 11.4 fusion.95
  665.4 131.0 %all-gather.31.cloned.1.call-done = bf16[1280,3840]{0,1:T(8,128)(2,1)} async-done(((bf16[1280,480]{0,1:T(8,128)(2,1)}), bf16[1280,3840]{0,1:T(8,128)(2,1)}) %all-gather.31.cloned.1.call-update) | async-done | bytes 9830416 | tf_op jit(solution)/shard_map/all_gather | solution.py:97
  796.4 8.2 constant_dynamic-update-slice_fusion.3
  804.7 134.4 %all-gather.33.cloned.1.call-done = bf16[1280,3840]{0,1:T(8,128)(2,1)} async-done(((bf16[1280,480]{0,1:T(8,128)(2,1)}), bf16[1280,3840]{0,1:T(8,128)(2,1)}) %all-gather.33.cloned.1.call-update) | async-done | bytes 9830416 | tf_op jit(solution)/shard_map/all_gather | solution.py:98
  939.1 8.3 constant_dynamic-update-slice_fusion.2
  947.3 16.1 all-gather.29.cloned.1.call-done
  963.5 17.8 fusion.94
  982.6 29.6 %reduce-scatter.27.cloned.1.call-done = f32[256,7680]{1,0:T(8,128)} async-done(((f32[512,7680]{1,0:T(8,128)}), f32[256,7680]{1,0:T(8,128)}) %reduce-scatter.27.cloned.1.call-update) | async-done | bytes 7864336 | tf_op jit(solution)/shard_map/reduce_scatter | solution.py:79
  1012.2 8.2 multiply_reduce_fusion
  1023.6 19.5 all-gather.41.cloned.1.call-done
  1043.1 16.6 convolution_convert_fusion.4
  1059.8 10.7 convolution_convert_fusion.6
  1070.7 16.1 reduce-scatter.33.cloned.1.call-done
  1091.6 21.1 reduce-scatter.29.cloned.1.call-done
  1118.7 24.3 all-gather.43.cloned.1.call-done
  1143.0 5.7 fusion.96
  1165.0 5.9 slice.655
  1170.9 5.9 slice.664
  1176.8 5.9 slice.657
  1182.7 5.1 fusion.76
  1196.3 6.0 slice.661
  1202.2 5.9 slice.659
  1347.8 5.9 slice.717
  1378.7 4.8 pad.280
  1383.5 4.9 pad.281
  1393.6 10.7 rev.14
  1404.3 10.7 rev.15
  1415.0 21.6 all-gather.2
  1436.7 17.9 all-gather.3
  1456.1 5.7 fusion.73
  1469.3 5.0 multiply_reduce_fusion.1
  1482.2 7.2 multiply_reduce_fusion.4
  1496.3 4.9 convolution_convert_fusion.3
  1501.7 5.3 all-gather.45.cloned.1.call-done
  1506.9 8.3 convolution_convert_fusion.5
  1516.5 9.9 convolution_convert_fusion.1
  1527.7 5.6 convolution_convert_fusion.2
  1536.6 5.7 copy.110
  1542.3 5.7 copy.112
  1549.4 17.6 convolution_convert_fusion
  1567.0 15.1 fusion.79
  1582.1 13.8 copy.114
  1596.0 13.8 copy.116
  1620.9 82.5 %all-reduce.73 = (f32[1280]{0:T(1024)}, f32[1280]{0:T(1024)}, f32[1280]{0:T(1024)}, f32[1280]{0:T(1024)}) all-reduce(f32[1280]{0:T(1024)S(1)} %get-tuple-element.327, f32[1280]{0:T(1024)S(1)} %copy-done.61, f32[1280]{0:T(1024)S(1)} %copy-done.60, f32[1280]{0:T(1024)S(1)} %copy-done.62), channel_id=1, replica_groups=mesh['dp'=8,'row'=2,'col'=2] {'dp','row'}, use_global_device_ids=true, to_apply=%region_21.22 | all-reduce | flops 5120 | bytes 40960 | tf_op jit(solution)/shard_map/psum | solution.py:326
  1704.9 81.2 %reduce-scatter.41.cloned.1.call-done = bf16[3840,160]{0,1:T(8,128)(2,1)} async-done(((bf16[3840,1280]{0,1:T(8,128)(2,1)}), bf16[3840,160]{0,1:T(8,128)(2,1)}) %reduce-scatter.41.cloned.1.call-update) | async-done | bytes 1228816 | tf_op jit(solution)/shard_map/reduce_scatter | solution.py:114
  1789.0 76.0 %reduce-scatter.43.cloned.1.call-done = bf16[160,1280]{1,0:T(8,128)(2,1)} async-done(((bf16[1280,1280]{1,0:T(8,128)(2,1)}), bf16[160,1280]{1,0:T(8,128)(2,1)}) %reduce-scatter.43.cloned.1.call-update) | async-done | bytes 409616
  1867.3 76.2 %reduce-scatter.45.cloned.1.call-done = bf16[160,1280]{1,0:T(8,128)(2,1)} async-done(((bf16[1280,1280]{1,0:T(8,128)(2,1)}), bf16[160,1280]{1,0:T(8,128)(2,1)}) %reduce-scatter.45.cloned.1.call-update) | async-done | bytes 409616
  1945.8 169.8 %reduce-scatter.47.cloned.1.call-done = bf16[480,1280]{1,0:T(8,128)(2,1)} async-done(((bf16[3840,1280]{1,0:T(8,128)(2,1)}), bf16[480,1280]{1,0:T(8,128)(2,1)}) %reduce-scatter.47.cloned.1.call-update) | async-done | bytes 1228816
  2119.1 168.9 %reduce-scatter.49.cloned.1.call-done = bf16[480,1280]{1,0:T(8,128)(2,1)} async-done(((bf16[3840,1280]{1,0:T(8,128)(2,1)}), bf16[480,1280]{1,0:T(8,128)(2,1)}) %reduce-scatter.49.cloned.1.call-update) | async-done | bytes 1228816
  2291.4 90.9 %all-reduce.77.cloned.1.call-done = (f32[1280]{0:T(1024)}, f32[1280]{0:T(1024)}, f32[4,1280]{1,0:T(4,128)}, f32[1280]{0:T(1024)}, f32[1280]{0:T(1024)}, /*index=...) async-done(((f32[1280]{0:T(1024)}, f32[1280]{0:T(1024)}, f32[4,1280]{1,0:T(4,128)}, f32[1280]{0:T(1024)}, f32[1280]{0:T(1024)}, /*index=5*/f32[1280]{0:T(1024)}, ...) | async-done | bytes 81936 | tf_op jit(solution)/shard_map/psum | solution.py:335
  2382.3 107.8 %all-reduce.79.cloned.1.call-done = (f32[5,256,256]{2,1,0:T(8,128)}, f32[5,256,256]{2,1,0:T(8,128)}) async-done(((f32[5,256,256]{2,1,0:T(8,128)}, f32[5,256,256]{2,1,0:T(8,128)}), (f32[5,256,256]{2,1,0:T(8,128)}, f32[5,256,256]{2,1,0:T(8,128)})) %all-reduce.79.cloned.1.call-update) | async-done | bytes 2621456 | tf_op jit(solution)/shard_map/psum | solution.py:335
  (693 shorter events, 521.1 us)
Async XLA Ops:
  7.2 183.2 %copy-start = (bf16[5,256,256]{2,1,0:T(8,128)(2,1)S(1)}, bf16[5,256,256]{2,1,0:T(8,128)(2,1)}, u32[]{:S(2)}) copy-start(bf16[5,256,256]{2,1,0:T(8,128)(2,1)} %param.37) | copy-start | bytes 1966084
  7.2 67.2 %all-gather.21.cloned.1.call-start = ((), (), s32[]{:S(2)}) async-start(), calls=%async_computation.15 | async-start | bytes 3686400 | tf_op jit(solution)/shard_map/all_gather | solution.py:94
  8.0 128.8 %all-gather.23.cloned.1.call-start = ((), (), s32[]{:S(2)}) async-start(), calls=%async_computation.16 | async-start | bytes 3686400 | tf_op jit(solution)/shard_map/all_gather | solution.py:95
  8.7 153.1 %all-gather.19.cloned.1.call-start = ((), (), s32[]{:S(2)}) async-start(), calls=%async_computation.14 | async-start | bytes 1966080 | tf_op jit(solution)/shard_map/all_gather | solution.py:78
  13.3 65.0 %copy-start.88 = (f32[256,1]{0,1:T(1,128)}, f32[256,1]{0,1:T(1,128)S(1)}, u32[]{:S(2)}) copy-start(f32[256,1]{0,1:T(1,128)S(1)} %get-tuple-element.380) | copy-start | bytes 3076
  13.3 65.0 %copy-start.38 = (f32[1280]{0:T(1024)}, f32[1280]{0:T(1024)S(1)}, u32[]{:S(2)}) copy-start(f32[1280]{0:T(1024)S(1)} %broadcast_add_fusion.1) | copy-start | bytes 15364
  14.4 169.8 %reduce-scatter.23.cloned.1.call-start = ((), (), s32[]{:S(2)}) async-start(), calls=%async_computation.17 | async-start | bytes 7864320 | tf_op jit(solution)/shard_map/reduce_scatter | solution.py:79
  171.0 13.2 copy-start.90
  171.0 275.2 %all-gather.27.cloned.1.call-start = ((), (), s32[]{:S(2)}) async-start(), calls=%async_computation.19 | async-start | bytes 3686400 | tf_op jit(solution)/shard_map/all_gather | solution.py:96
  171.6 282.2 %all-gather.25.cloned.1.call-start = ((), (), s32[]{:S(2)}) async-start(), calls=%async_computation.18 | async-start | bytes 1966080 | tf_op jit(solution)/shard_map/all_gather | solution.py:83
  171.7 17.1 copy-start.100
  171.7 17.1 copy-start.102
  171.7 17.0 copy-start.104
  171.7 26.2 %copy-start.93 = (pred[256]{0:T(512)(128)(4,1)}, pred[256]{0:T(512)(128)(4,1)S(1)}, u32[]{:S(2)}) copy-start(pred[256]{0:T(512)(128)(4,1)S(1)} %get-tuple-element.482) | copy-start | bytes 772
  171.8 16.9 copy-start.48
  171.8 16.9 copy-start.50
  171.8 16.9 copy-start.52
  171.8 16.9 copy-start.54
  171.9 16.9 copy-start.91
  185.6 3.1 collective-permute-start
  416.4 24.6 copy-start.65
  445.9 37.8 %reduce-scatter.25.cloned.1.call-start = ((), (), s32[]{:S(2)}) async-start(), calls=%async_computation.20 | async-start | bytes 1966080 | tf_op jit(solution)/shard_map/reduce_scatter | solution.py:86
  459.1 50.4 %all-gather.39.cloned.1.call-start = ((), (), s32[]{:S(2)}) async-start(), calls=%async_computation.28 | async-start | bytes 1966080 | tf_op jit(solution)/shard_map/all_gather | solution.py:78
  459.8 194.1 %all-gather.37.cloned.1.call-start = ((), (), s32[]{:S(2)}) async-start(), calls=%async_computation.26 | async-start | bytes 11059200 | tf_op jit(solution)/shard_map/all_gather | solution.py:99
  460.6 23.1 copy-start.37
  460.6 335.8 %all-gather.31.cloned.1.call-start = ((), (), s32[]{:S(2)}) async-start(), calls=%async_computation.22 | async-start | bytes 11059200 | tf_op jit(solution)/shard_map/all_gather | solution.py:97
  461.2 477.9 %all-gather.33.cloned.1.call-start = ((), (), s32[]{:S(2)}) async-start(), calls=%async_computation.23 | async-start | bytes 11059200 | tf_op jit(solution)/shard_map/all_gather | solution.py:98
  461.9 501.5 %all-gather.29.cloned.1.call-start = ((), (), s32[]{:S(2)}) async-start(), calls=%async_computation.21 | async-start | bytes 1966080 | tf_op jit(solution)/shard_map/all_gather | solution.py:78
  489.8 492.7 %reduce-scatter.31.cloned.1.call-start = ((), (), s32[]{:S(2)}) async-start(), calls=%async_computation.29 | async-start | bytes 11796480 | tf_op jit(solution)/shard_map/reduce_scatter | solution.py:79
  665.4 346.8 %reduce-scatter.27.cloned.1.call-start = ((), (), s32[]{:S(2)}) async-start(), calls=%async_computation.24 | async-start | bytes 23592960 | tf_op jit(solution)/shard_map/reduce_scatter | solution.py:79
  981.3 30.9 %copy-start.86 = (f32[3840]{0:T(1024)S(1)}, f32[3840]{0:T(1024)}, u32[]{:S(2)}) copy-start(f32[3840]{0:T(1024)} %param.44) | copy-start | bytes 46084
  981.3 30.9 %copy-start.87 = (f32[3840]{0:T(1024)S(1)}, f32[3840]{0:T(1024)}, u32[]{:S(2)}) copy-start(f32[3840]{0:T(1024)} %param.46) | copy-start | bytes 46084
  981.3 61.8 %all-gather.41.cloned.1.call-start = ((), (), s32[]{:S(2)}) async-start(), calls=%async_computation.30 | async-start | bytes 11796480 | tf_op jit(solution)/shard_map/all_gather | solution.py:83
  1022.6 37.3 %all-gather.35.cloned.1.call-start = ((), (), s32[]{:S(2)}) async-start(), calls=%async_computation.25 | async-start | bytes 5898240 | tf_op jit(solution)/shard_map/all_gather | solution.py:83
  1023.2 63.6 %reduce-scatter.33.cloned.1.call-start = ((), (), s32[]{:S(2)}) async-start(), calls=%async_computation.31 | async-start | bytes 1966080 | tf_op jit(solution)/shard_map/reduce_scatter | solution.py:86
  1059.8 52.9 %reduce-scatter.29.cloned.1.call-start = ((), (), s32[]{:S(2)}) async-start(), calls=%async_computation.27 | async-start | bytes 1966080 | tf_op jit(solution)/shard_map/reduce_scatter | solution.py:86
  1070.6 42.1 %copy-start.92 = (f32[1280]{0:T(1024)S(1)}, f32[1280]{0:T(1024)}, u32[]{:S(2)}) copy-start(f32[1280]{0:T(1024)} %param.48) | copy-start | bytes 15364
  1070.6 72.4 %all-gather.43.cloned.1.call-start = ((), (), s32[]{:S(2)}) async-start(), calls=%async_computation.32 | async-start | bytes 1966080 | tf_op jit(solution)/shard_map/all_gather | solution.py:78
  1118.6 64.1 %reduce-scatter.35.cloned.1.call-start = ((), (), s32[]{:S(2)}) async-start(), calls=%async_computation.33 | async-start | bytes 3932160 | tf_op jit(solution)/shard_map/reduce_scatter | solution.py:79
  1148.8 358.1 %all-gather.45.cloned.1.call-start = ((), (), s32[]{:S(2)}) async-start(), calls=%async_computation.34 | async-start | bytes 3932160 | tf_op jit(solution)/shard_map/all_gather | solution.py:83
  1170.9 11.8 copy-start.66
  1278.2 14.6 copy-start.74
  1278.2 14.6 copy-start.75
  1278.2 14.7 copy-start.56
  1278.2 14.8 copy-start.57
  1278.2 14.8 copy-start.71
  1281.0 14.7 copy-start.46
  1281.0 14.7 copy-start.47
  1283.7 17.4 copy-start.35
  1283.7 17.4 copy-start.36
  1414.9 41.2 %copy-start.41 = (f32[1280]{0:T(1024)S(1)}, f32[1280]{0:T(1024)}, u32[]{:S(2)}) copy-start(f32[1280]{0:T(1024)} %param.38) | copy-start | bytes 15364
  1489.9 3.1 collective-permute-start.1
  1495.0 119.8 %reduce-scatter.39.cloned.1.call-start = ((), (), s32[]{:S(2)}) async-start(), calls=%async_computation.36 | async-start | bytes 3686400 | tf_op jit(solution)/shard_map/reduce_scatter | solution.py:114
  1501.2 115.7 %reduce-scatter.37.cloned.1.call-start = ((), (), s32[]{:S(2)}) async-start(), calls=%async_computation.35 | async-start | bytes 1966080 | tf_op jit(solution)/shard_map/reduce_scatter | solution.py:86
  1515.2 270.9 %reduce-scatter.41.cloned.1.call-start = ((), (), s32[]{:S(2)}) async-start(), calls=%async_computation.37 | async-start | bytes 11059200 | tf_op jit(solution)/shard_map/reduce_scatter | solution.py:114
  1526.4 338.5 %reduce-scatter.43.cloned.1.call-start = ((), (), s32[]{:S(2)}) async-start(), calls=%async_computation.38 | async-start | bytes 3686400
  1542.3 401.2 %reduce-scatter.45.cloned.1.call-start = ((), (), s32[]{:S(2)}) async-start(), calls=%async_computation.39 | async-start | bytes 3686400
  1548.0 567.6 %reduce-scatter.47.cloned.1.call-start = ((), (), s32[]{:S(2)}) async-start(), calls=%async_computation.40 | async-start | bytes 11059200
  1595.9 692.1 %reduce-scatter.49.cloned.1.call-start = ((), (), s32[]{:S(2)}) async-start(), calls=%async_computation.41 | async-start | bytes 11059200
  1609.8 772.5 %all-reduce.77.cloned.1.call-start = ((), (), s32[]{:S(2)}) async-start(), calls=%async_computation.42 | async-start | bytes 204800 | tf_op jit(solution)/shard_map/psum | solution.py:335
  1613.2 876.9 %all-reduce.79.cloned.1.call-start = ((), (), s32[]{:S(2)}) async-start(), calls=%async_computation.43 | async-start | bytes 5242880 | tf_op jit(solution)/shard_map/psum | solution.py:335
  1614.8 88.6 %copy-start.6 = (f32[256,1280]{1,0:T(8,128)S(1)}, f32[256,1280]{1,0:T(8,128)}, u32[]{:S(2)}) copy-start(f32[256,1280]{1,0:T(8,128)} %copy-done.5) | copy-start | bytes 3932164
  1614.8 88.6 %copy-start.108 = (f32[256,1]{0,1:T(1,128)S(1)}, f32[256,1]{0,1:T(1,128)}, u32[]{:S(2)}) copy-start(f32[256,1]{0,1:T(1,128)} %get-tuple-element.379) | copy-start | bytes 3076
  1616.9 86.6 %copy-start.26 = (bf16[256,1280]{1,0:T(8,128)(2,1)S(1)}, bf16[256,1280]{1,0:T(8,128)(2,1)}, u32[]{:S(2)}) copy-start(bf16[256,1280]{1,0:T(8,128)(2,1)} %reduce-scatter.37.cloned.1.call-done) | copy-start | bytes 1966084
  (81 other events, 325.1 us)
Sparse Core Ops, SparseCore 0:
  10.2 64.1 all-gather.20
  76.6 60.1 all-gather.22
  138.9 22.9 all-gather.18
  171.1 13.0 reduce-scatter.22
  186.2 62.7 all-gather.26
  446.0 7.7 all-gather.24
  459.2 24.4 reduce-scatter.24
  485.2 24.2 all-gather.38
  511.7 142.2 all-gather.36
  656.0 140.3 all-gather.30
  798.6 140.3 all-gather.32
  941.0 22.3 all-gather.28
  965.8 16.7 reduce-scatter.30
  984.8 27.3 reduce-scatter.26
  1022.7 20.3 all-gather.40
  1045.1 14.4 all-gather.34
  1062.2 24.4 reduce-scatter.32
  1089.4 23.2 reduce-scatter.28
  1118.7 24.2 all-gather.42
  1148.9 10.4 reduce-scatter.34
  1495.1 11.7 all-gather.44
  1510.5 77.3 reduce-scatter.38
  1590.7 22.2 reduce-scatter.36
  1616.5 169.5 reduce-scatter.40
  1789.7 75.2 reduce-scatter.42
  1868.4 75.0 reduce-scatter.44
  1947.0 168.6 reduce-scatter.46
  2119.3 168.6 reduce-scatter.48
  2294.5 87.7 all-reduce.76
  2386.4 103.6 all-reduce.78
where the time goes:
time: 2530 us; the launch traced here: 2510 us
  waiting for transfers between devices  1520 us (60%)
  local copies, waits for them, and re-layouts  477 us (19%)
  other arithmetic  179 us (7%)
  blocking collectives  174 us (7%)
  matrix products  134 us (5%)
    unnamed x34, waiting for transfers between devices  496 us
    psum x2, waiting for transfers between devices, on_device(): lax.psum((jnp.sum(delta_branch, axis=0), jnp.sum(delta_mixer, axis=0), gr...  199 us
    all_gather x1, waiting for transfers between devices, fetch_weights(): lax.all_gather(down_weight, 'dp', axis=1, tiled=True)  144 us
    all_gather x1, waiting for transfers between devices, fetch_weights(): lax.all_gather(up_weight, 'dp', axis=1, tiled=True)  134 us
    all_gather x1, waiting for transfers between devices, fetch_weights(): lax.all_gather(gate_weight, 'dp', axis=1, tiled=True)  131 us
    slice x57, local copies, waits for them, and re-layouts, on_device(): lax.associative_scan(affine, (retain_next[::-1], delta_state[::-1]), axis=0)  127 us
    slice x52, local copies, waits for them, and re-layouts, on_device(): lax.associative_scan(affine, (retain, source), axis=0)  91.3 us
    unnamed x255, local copies, waits for them, and re-layouts  82.8 us
  transfers between devices with their start and end apart: 32, of which 27 were waited for; matrix products, arithmetic and copies ran while one was open for 19% of the time, Pallas kernels for 0%

commit v1 on v0

v1 whole, which is shorter than its diff:
```python
import jax
import jax.numpy as jnp
from jax import lax
from jax.experimental import pallas as pl
from jax.experimental.pallas import tpu as pltpu
from jax.sharding import Mesh, PartitionSpec as P

D = 2560
CONV = 4
LEN = 4096
EPSILON = 1e-06
SQRT_FLOOR = 0.0001
TEAM = 4
NT = (((1,), (1,)), ((), ()))
TN = (((0,), (0,)), ((), ()))
F32 = jnp.float32
BF16 = jnp.bfloat16
DP = ("t", "f")
ORDER = ("t", "f", "col")


def dot_nn(a, b):
    return jnp.dot(a, b, preferred_element_type=F32)


def dot_nt(a, b):
    return lax.dot_general(a, b, NT, preferred_element_type=F32)


def dot_tn(a, b):
    return lax.dot_general(a, b, TN, preferred_element_type=F32)


def gather(x, axes, dim):
    return lax.all_gather(x, axes, axis=dim, tiled=True)


def scatter(x, axes, dim):
    return lax.psum_scatter(x, axes, scatter_dimension=dim, tiled=True)


def swap(x, axes, split, concat):
    return lax.all_to_all(x, axes, split_axis=split, concat_axis=concat, tiled=True)


def from_behind(x, axis, by):
    peers = lax.axis_size(axis)
    pairs = [(i, i + by) for i in range(peers) if 0 <= i + by < peers]
    return lax.ppermute(x, axis, pairs)


def scan_rows(retain, source, backward):
    rows, width = retain.shape
    tiles = rows // 8

    def kernel(r_ref, s_ref, c_ref, h_ref):
        row = lax.broadcasted_iota(jnp.int32, (8, width), 0)

        def step(i, carry):
            decay, state = carry
            at = pl.ds(pl.multiple_of(8 * (tiles - 1 - i if backward else i), 8), 8)
            r, s = r_ref[at, :], s_ref[at, :]
            for by in (1, 2, 4):
                keep = row < 8 - by if backward else row >= by
                shift = 8 - by if backward else by
                r_by = jnp.where(keep, pltpu.roll(r, shift, 0), 1.0)
                s_by = jnp.where(keep, pltpu.roll(s, shift, 0), 0.0)
                s = r * s_by + s
                r = r * r_by
            s = s + r * state
            r = r * decay
            c_ref[at, :] = r
            h_ref[at, :] = s
            end = 0 if backward else 7
            return r[end : end + 1, :], s[end : end + 1, :]

        lax.fori_loop(0, tiles, step, (jnp.ones((1, width), F32), jnp.zeros((1, width), F32)))

    return pl.pallas_call(
        kernel,
        out_shape=(jax.ShapeDtypeStruct((rows, width), F32),) * 2,
        in_specs=[pl.BlockSpec(memory_space=pltpu.VMEM)] * 2,
        out_specs=(pl.BlockSpec(memory_space=pltpu.VMEM),) * 2,
        name="scan_back" if backward else "scan_rows",
    )(retain, source)


def carry_in(decay, state, backward):
    count, mine = lax.axis_size(ORDER), lax.axis_index(ORDER)
    ends = lax.all_gather(jnp.stack([decay, state]), ORDER)
    running = jnp.zeros_like(state)
    for i in range(count - 1):
        peer = count - 1 - i if backward else i
        ahead = peer > mine if backward else peer < mine
        running = jnp.where(ahead, ends[peer, 0] * running + ends[peer, 1], running)
    return running


def gelu_tanh(values):
    return jax.nn.gelu(values, approximate=True)


def gates_of(decay_pre, input_pre, decay_param, conv_low, starts):
    rate_gate = jax.nn.sigmoid(decay_pre)
    in_gate = jax.nn.sigmoid(input_pre)
    log_decay = -8.0 * jax.nn.softplus(decay_param) * rate_gate
    retain = jnp.where(starts, 0.0, jnp.exp(log_decay))
    multiplier = jnp.where(
        starts, 1.0, jnp.sqrt(jnp.maximum(-jnp.expm1(2.0 * log_decay), SQRT_FLOOR))
    )
    return (retain, multiplier * in_gate * conv_low)


def feature_total(values):
    return lax.psum(values, "col")


def normalize(values, scale_vec):
    inverse = lax.rsqrt(
        feature_total(jnp.sum(values * values, axis=1, keepdims=True)) / D + EPSILON
    )
    return (values * inverse * (1.0 + scale_vec), inverse)


def normalize_back(gradient, values, inverse, scale_vec):
    weighted = gradient * (1.0 + scale_vec)
    scale_grad = jnp.sum(gradient * values * inverse, axis=0)
    inner_sum = feature_total(jnp.sum(weighted * values, axis=1, keepdims=True))
    return (inverse * weighted - values * inverse**3 * inner_sum / D, scale_grad)


def to_tokens(block):
    rows = gather(block, "row", 0)
    both = swap(rows.reshape(2, block.shape[0], block.shape[1]), "col", 0, 2)
    return rows, both[0]


def to_stream(partial):
    tokens, width = partial.shape
    halves = jnp.stack([partial[:, : width // 2], partial[:, width // 2 :]])
    return scatter(swap(halves, "col", 0, 1)[0], "row", 0)


def square_down(down_weight):
    width = down_weight.shape[1]
    share = down_weight.shape[0] // (2 * TEAM)
    pieces = down_weight.T.reshape(width, 2 * TEAM, share).transpose(1, 0, 2)
    pieces = swap(pieces, ("t", "col"), 0, 0)
    every = lax.all_gather(pieces, "f").reshape(-1, TEAM, 2, width, share)
    return every.transpose(2, 1, 0, 3, 4).reshape(-1, share)


def square_down_back(grad, fleet):
    share = grad.shape[1]
    every = grad.reshape(2, TEAM, fleet, -1, share).transpose(2, 1, 0, 3, 4)
    summed = scatter(every.reshape(fleet, 2 * TEAM, -1, share), "f", 0)[0]
    pieces = swap(summed, ("t", "col"), 0, 0)
    return pieces.transpose(0, 2, 1).reshape(2 * TEAM * share, -1)


def ffn_columns(weight):
    block = gather(weight.T, "f", 0)
    return swap(block, "col", 0, 1)


def ffn_columns_back(grad):
    return scatter(swap(grad, "col", 1, 0), "f", 0).T


def on_device(
    stream,
    scale_first,
    branch_weight,
    branch_bias,
    mixer_weight,
    mixer_bias,
    conv_weight,
    conv_bias,
    decay_weight,
    decay_bias,
    input_weight,
    input_bias,
    decay_param,
    output_weight,
    output_bias,
    scale_second,
    gate_weight,
    gate_bias,
    up_weight,
    up_bias,
    down_weight,
    down_bias,
    cotangent,
):
    fleet = lax.axis_size("f")
    mixer_t = gather(gather(mixer_weight.T, DP, 0), "col", 1)
    branch_t = gather(gather(branch_weight.T, DP, 0), "col", 1)
    output_t = gather(gather(output_weight.T, DP, 0), "col", 0)
    inner = mixer_t.shape[0]
    stream_wide = stream.astype(F32)
    normed_first, inverse_first = normalize(stream_wide, scale_first)
    first_rows, first_all = to_tokens(normed_first.astype(BF16))
    mixer_pre = dot_nt(first_all, mixer_t) + mixer_bias
    branch_pre = dot_nt(first_all, branch_t) + branch_bias
    branch_act, branch_back = jax.vjp(gelu_tanh, branch_pre)

    steps = mixer_pre.shape[0]
    first_token = lax.axis_index(ORDER) * steps
    position = (first_token + jnp.arange(steps, dtype=jnp.int32)) % LEN
    margin = CONV - 1
    left_edge = from_behind(mixer_pre[steps - margin :], ORDER, 1)
    padded = jnp.concatenate([left_edge, mixer_pre], axis=0)
    conv_out = conv_bias + jnp.zeros_like(mixer_pre)
    for offset in range(CONV):
        in_reach = (position >= offset)[:, None]
        conv_out = conv_out + jnp.where(
            in_reach, conv_weight[offset] * padded[margin - offset : margin - offset + steps], 0.0
        )
    conv_low = conv_out.astype(BF16)
    conv_wide = conv_low.astype(F32)
    heads, block = decay_weight.shape[0], decay_weight.shape[1]
    conv_heads = conv_low.reshape(steps, heads, block)
    parts = [conv_low[:, h * block : (h + 1) * block] for h in range(heads)]
    decay_pre = jnp.concatenate([dot_nn(x, decay_weight[h]) for h, x in enumerate(parts)], 1) + decay_bias
    input_pre = jnp.concatenate([dot_nn(x, input_weight[h]) for h, x in enumerate(parts)], 1) + input_bias
    starts = (position == 0)[:, None]

    def gate_values(decay_in, input_in, param_in, conv_in):
        return gates_of(decay_in, input_in, param_in, conv_in, starts)

    (retain, source), gate_back = jax.vjp(gate_values, decay_pre, input_pre, decay_param, conv_wide)
    cumulative, local_state = scan_rows(retain, source, False)
    state_in = carry_in(cumulative[-1], local_state[-1], False)
    states = local_state + cumulative * state_in
    mixed_low = (states * branch_act).astype(BF16)
    out_proj = to_stream(dot_nt(mixed_low, output_t).astype(BF16)).astype(F32)
    first_out = stream_wide + out_proj + output_bias
    normed_second, inverse_second = normalize(first_out, scale_second)

    gate_t = ffn_columns(gate_weight)
    up_t = ffn_columns(up_weight)
    down_t = square_down(down_weight)
    share = gate_t.shape[0]
    mine = (lax.axis_index("t") * 2 + lax.axis_index("col")) * share
    gate_b = lax.dynamic_slice(gate_bias, (mine,), (share,))
    up_b = lax.dynamic_slice(up_bias, (mine,), (share,))

    def everywhere(x):
        return gather(gather(x, ("t", "row"), 0), "col", 1)

    def home(x):
        return scatter(scatter(x.astype(BF16), "col", 1), ("t", "row"), 0).astype(F32)

    second_all = everywhere(normed_second.astype(BF16))
    cot_all = everywhere(cotangent)
    gate_pre = dot_nt(second_all, gate_t) + gate_b
    up_pre = dot_nt(second_all, up_t) + up_b
    hidden, hidden_back = jax.vjp(lambda g, u: gelu_tanh(g) * u, gate_pre, up_pre)
    hidden_low = hidden.astype(BF16)
    delta_hidden = dot_nn(cot_all, down_t)
    delta_gate, delta_up = hidden_back(delta_hidden)
    gate_low, up_low = delta_gate.astype(BF16), delta_up.astype(BF16)
    delta_second = home(dot_nn(gate_low, gate_t) + dot_nn(up_low, up_t))
    down_proj = home(dot_nt(hidden_low, down_t))
    result = (first_out + down_proj + down_bias).astype(BF16)
    delta_result = cotangent.astype(F32)
    grad_gate = ffn_columns_back(dot_tn(gate_low, second_all).astype(BF16)).astype(F32)
    grad_up = ffn_columns_back(dot_tn(up_low, second_all).astype(BF16)).astype(F32)
    grad_down = square_down_back(dot_tn(cot_all, hidden_low).astype(BF16), fleet).astype(F32)

    norm_second_part, grad_scale_second = normalize_back(
        delta_second, first_out, inverse_second, scale_second
    )
    delta_first = delta_result + norm_second_part
    out_rows, out_all = to_tokens(delta_first.astype(BF16))
    delta_mixed = dot_nn(out_all, output_t)
    grad_output = scatter(dot_tn(out_rows, gather(mixed_low, "col", 0)).astype(BF16), DP, 0)
    delta_state = delta_mixed * branch_act
    (delta_branch,) = branch_back(delta_mixed * states)
    branch_low = delta_branch.astype(BF16)
    grad_branch = scatter(dot_tn(gather(branch_low, "col", 0), first_rows).astype(BF16), DP, 0)
    ones_row = jnp.ones((1, inner), F32)
    retain_next = jnp.concatenate([retain[1:], ones_row], axis=0)
    suffix, local_back = scan_rows(retain_next, delta_state, True)
    back_in = carry_in(retain[0] * suffix[0], retain[0] * local_back[0], True)
    back_state = local_back + suffix * back_in
    state_prev = jnp.concatenate([state_in[None], states[:-1]], axis=0)
    delta_decay_pre, delta_input_pre, grad_decay_param, delta_conv = gate_back(
        (back_state * state_prev, back_state)
    )
    decay_low = delta_decay_pre.astype(BF16)
    input_low = delta_input_pre.astype(BF16)

    def split(x):
        return [x[:, h * block : (h + 1) * block] for h in range(heads)]

    grad_decay_weight = jnp.stack([dot_tn(a, b) for a, b in zip(parts, split(decay_low))])
    grad_input_weight = jnp.stack([dot_tn(a, b) for a, b in zip(parts, split(input_low))])
    delta_conv = delta_conv + jnp.concatenate(
        [dot_nt(a, decay_weight[h]) for h, a in enumerate(split(decay_low))], 1
    )
    delta_conv = delta_conv + jnp.concatenate(
        [dot_nt(a, input_weight[h]) for h, a in enumerate(split(input_low))], 1
    )
    delta_padded = jnp.zeros_like(padded)
    conv_grads = []
    for offset in range(CONV):
        in_reach = (position >= offset)[:, None]
        masked = jnp.where(in_reach, delta_conv, 0.0)
        conv_grads.append(
            jnp.sum(masked * padded[margin - offset : margin - offset + steps], axis=0)
        )
        delta_padded = delta_padded + jnp.pad(
            masked * conv_weight[offset], ((margin - offset, offset), (0, 0))
        )
    grad_conv_weight = jnp.stack(conv_grads, axis=0)
    right_edge = from_behind(delta_padded[:margin], ORDER, -1)
    delta_mixer = delta_padded[margin:] + jnp.pad(right_edge, ((steps - margin, 0), (0, 0)))
    mixer_low = delta_mixer.astype(BF16)
    grad_mixer = scatter(dot_tn(gather(mixer_low, "col", 0), first_rows).astype(BF16), DP, 0)
    delta_normed_first = to_stream(
        (dot_nn(branch_low, branch_t) + dot_nn(mixer_low, mixer_t)).astype(BF16)
    ).astype(F32)
    norm_first_part, grad_scale_first = normalize_back(
        delta_normed_first, stream_wide, inverse_first, scale_first
    )
    grad_stream = delta_first + norm_first_part

    stream_sums = lax.psum(
        jnp.stack(
            [
                grad_scale_first,
                grad_scale_second,
                jnp.sum(delta_first, axis=0),
                jnp.sum(delta_result, axis=0),
            ]
        ),
        ("t", "f", "row"),
    )

    def spread(x):
        return lax.dynamic_update_slice(jnp.zeros_like(gate_bias), x, (mine,))

    small = [
        jnp.sum(delta_branch, axis=0),
        jnp.sum(delta_mixer, axis=0),
        jnp.sum(delta_conv, axis=0),
        jnp.sum(delta_decay_pre, axis=0),
        jnp.sum(delta_input_pre, axis=0),
        grad_decay_param,
        spread(jnp.sum(delta_gate, axis=0)),
        spread(jnp.sum(delta_up, axis=0)),
        grad_conv_weight.reshape(-1),
    ]
    sizes = [x.shape[0] for x in small]
    total = lax.psum(jnp.concatenate(small), ORDER)
    sums, at = [], 0
    for size in sizes:
        sums.append(total[at : at + size])
        at += size
    grad_decay_weight, grad_input_weight = lax.psum((grad_decay_weight, grad_input_weight), ORDER)
    return (
        result,
        grad_stream,
        stream_sums[0],
        grad_branch.T.astype(F32),
        sums[0],
        grad_mixer.T.astype(F32),
        sums[1],
        sums[8].reshape(CONV, inner),
        sums[2],
        grad_decay_weight,
        sums[3],
        grad_input_weight,
        sums[4],
        sums[5],
        grad_output.T.astype(F32),
        stream_sums[2],
        stream_sums[1],
        grad_gate,
        sums[6],
        grad_up,
        sums[7],
        grad_down,
        stream_sums[3],
    )


def solution(mesh):
    shape = mesh.devices.shape
    names = mesh.axis_names
    fleet = mesh.shape["dp"] // TEAM
    at = names.index("dp")
    split_mesh = Mesh(
        mesh.devices.reshape(shape[:at] + (TEAM, fleet) + shape[at + 1 :]),
        names[:at] + DP + names[at + 1 :],
    )
    tokens, fan_in = P((*DP, "row"), "col"), P("col", ("row", *DP))
    fan_out, inner, wide = P("row", ("col", *DP)), P("row"), P("col")
    heads = P("row", None, None)
    return jax.shard_map(
        on_device,
        mesh=split_mesh,
        in_specs=(
            tokens, wide, fan_in, inner, fan_in, inner, P(None, "row"), inner,
            heads, inner, heads, inner, inner, fan_out, wide, wide,
            fan_in, inner, fan_in, inner, fan_out, wide, tokens,
        ),
        out_specs=(
            tokens, tokens, wide, fan_in, inner, fan_in, inner, P(None, "row"), inner,
            heads, inner, heads, inner, inner, fan_out, wide, wide,
            fan_in, inner, fan_in, inner, fan_out, wide,
        ),
        check_vma=False,
    )
```

time: 2530 us -> 1610 us (0.64)
  waiting for transfers between devices: 1520 us -> 1060 us
  local copies, waits for them, and re-layouts: 477 us -> 58.3 us
  other arithmetic: 179 us -> 51.3 us
  blocking collectives: 174 us -> 241 us
    unnamed x34 -> x31, waiting for transfers between devices: 496 us -> 4.21 us
    reduce_scatter x10 -> x12, waiting for transfers between devices: 183 us -> 458 us  [scatter(): return lax.psum_scatter(x, axes, scatter_dimension=dim, tiled=True)]
    slice x114 -> x12, local copies, waits for them, and re-layouts: 238 us -> 9.27 us  [the longest x4 4.21 us: on_device(): sums.append(total[at:at + size])]
    all_gather x14 -> x18, waiting for transfers between devices: 642 us -> 498 us  [the longest x17 466 us: gather(): return lax.all_gather(x, axes, axis=dim, tiled=True)]
    all_to_all x0 -> x9, blocking collectives: none -> 107 us  [swap(): lax.all_to_all(x, axes, split_axis=split, concat_axis=concat, tiled=True)]
    pad x56 -> x0, local copies, waits for them, and re-layouts: 104 us -> none  [the longest x28 52.4 us: on_device(): lax.associative_scan(affine, (retain_next[::-1], delta_state[::-1]), axis=0)]
    psum x2 -> x1, waiting for transfers between devices: 199 us -> 96.4 us  [on_device(): total = lax.psum(jnp.concatenate(small), ORDER)]
    unnamed x255 -> x139, local copies, waits for them, and re-layouts: 82.8 us -> 12.6 us
  transfers between devices with their start and end apart: 32 -> 34, of which waited for: 27 -> 25; matrix products, arithmetic and copies ran while one was open for 19% -> 12% of each run, Pallas kernels for 0% -> 1%
where the time goes in v1:
time: 1610 us; the launch traced here: 1600 us
  waiting for transfers between devices  1060 us (66%)
  blocking collectives  241 us (15%)
  matrix products  158 us (10%)
  local copies, waits for them, and re-layouts  58.3 us (4%)
  other arithmetic  51.3 us (3%)
  between operations  16.1 us (1%)
    all_gather x17, waiting for transfers between devices, gather(): return lax.all_gather(x, axes, axis=dim, tiled=True)  466 us
    reduce_scatter x12, waiting for transfers between devices, scatter(): return lax.psum_scatter(x, axes, scatter_dimension=dim, tiled=True)  458 us
    all_to_all x9, blocking collectives, swap(): lax.all_to_all(x, axes, split_axis=split, concat_axis=concat, tiled=True)  107 us
    psum x1, waiting for transfers between devices, on_device(): total = lax.psum(jnp.concatenate(small), ORDER)  96.4 us
    psum x1, blocking collectives, on_device(): lax.psum(jnp.stack([grad_scale_first, grad_scale_second, jnp.sum(delta_fi...  77.4 us
    dot_general x16, matrix products, dot_nn(): return jnp.dot(a, b, preferred_element_type=F32)  62.6 us
    dot_general x16, matrix products, dot_nt(): return lax.dot_general(a, b, NT, preferred_element_type=F32)  47.9 us
    dot_general x16, matrix products, dot_tn(): return lax.dot_general(a, b, TN, preferred_element_type=F32)  47.5 us
  transfers between devices with their start and end apart: 34, of which 25 were waited for; matrix products, arithmetic and copies ran while one was open for 12% of the time, Pallas kernels for 1%

profile of v1, /device:TPU:0, one launch (start us, length us, event | category | flops | bytes accessed | tf_op | source)
XLA Modules:
  0.0 1601.4 jit_solution(18156588728072633907)
XLA Ops:
  14.0 60.4 %all-gather.26.cloned.1.call-done = bf16[1280,1280]{1,0:T(8,128)(2,1)} async-done(((bf16[160,1280]{1,0:T(8,128)(2,1)}), bf16[1280,1280]{1,0:T(8,128)(2,1)}) %all-gather.26.cloned.1.call-update) | async-done | bytes 3276816 | tf_op jit(solution)/shard_map/all_gather | solution.py:35
  74.5 62.3 %all-gather.30.cloned.1.call-done = bf16[1280,1280]{1,0:T(8,128)(2,1)} async-done(((bf16[160,1280]{1,0:T(8,128)(2,1)}), bf16[1280,1280]{1,0:T(8,128)(2,1)}) %all-gather.30.cloned.1.call-update) | async-done | bytes 3276816 | tf_op jit(solution)/shard_map/all_gather | solution.py:35
  136.8 62.3 %all-gather.34.cloned.1.call-done = bf16[1280,1280]{1,0:T(8,128)(2,1)} async-done(((bf16[160,1280]{1,0:T(8,128)(2,1)}), bf16[1280,1280]{1,0:T(8,128)(2,1)}) %all-gather.34.cloned.1.call-update) | async-done | bytes 3276816 | tf_op jit(solution)/shard_map/all_gather | solution.py:35
  199.9 24.1 %all-gather.24.cloned.1.call-done = bf16[512,1280]{1,0:T(8,128)(2,1)} async-done(((bf16[256,1280]{1,0:T(8,128)(2,1)}), bf16[512,1280]{1,0:T(8,128)(2,1)}) %all-gather.24.cloned.1.call-update) | async-done | bytes 1310736 | tf_op jit(solution)/shard_map/all_gather | solution.py:35
  225.6 5.6 all_to_all.134
  231.3 11.4 all-gather.28.cloned.1.call-done
  242.6 5.2 convolution_add_fusion.2
  257.6 5.1 scan_rows.1
  264.3 23.7 %all-gather.3 = f32[16,2,1280]{2,1,0:T(2,128)S(1)} all-gather(f32[1,2,1280]{2,1,0:T(2,128)S(1)} %maximum_bitcast_fusion), channel_id=2, replica_groups=mesh['t'=4,'f'=2,'row'=2,'col'=2] {'t','f','col'}, dimensions={0}, use_global_device_ids=true | all-gather | bytes 174080 | tf_op jit(solution)/shard_map/all_gather | solution.py:90
  288.5 7.6 multiply_convert_fusion.3
  296.2 5.0 convolution_convert_fusion.7
  301.4 5.6 all_to_all.135
  307.7 20.0 %reduce-scatter.13.cloned.1.call-done = bf16[256,1280]{1,0:T(8,128)(2,1)} async-done(((bf16[512,1280]{1,0:T(8,128)(2,1)}), bf16[256,1280]{1,0:T(8,128)(2,1)}) %reduce-scatter.13.cloned.1.call-update) | async-done | bytes 655376 | tf_op jit(solution)/shard_map/reduce_scatter | solution.py:39
  335.5 4.1 reshape.706
  341.4 53.9 %all_to_all.136 = bf16[8,160,480]{2,1,0:T(8,128)(2,1)} all-to-all(bf16[8,160,480]{2,1,0:T(8,128)(2,1)S(1)} %copy.201), channel_id=1, replica_groups=mesh['t'=4,'f'=2,'row'=2,'col'=2] {'t','col'}, dimensions={0} | all-to-all | bytes 2457600 | tf_op jit(solution)/shard_map/all_to_all | solution.py:43
  395.3 47.3 %all-gather.38.cloned.1.call-done = bf16[2048,1280]{1,0:T(8,128)(2,1)} async-done(((bf16[256,1280]{1,0:T(8,128)(2,1)}), bf16[2048,1280]{1,0:T(8,128)(2,1)}) %all-gather.38.cloned.1.call-update) | async-done | bytes 5242896 | tf_op jit(solution)/shard_map/all_gather | solution.py:35
  442.7 86.1 %all-gather.46.cloned.1.call-done = bf16[2048,1280]{1,0:T(8,128)(2,1)} async-done(((bf16[256,1280]{1,0:T(8,128)(2,1)}), bf16[2048,1280]{1,0:T(8,128)(2,1)}) %all-gather.46.cloned.1.call-update) | async-done | bytes 5242896 | tf_op jit(solution)/shard_map/all_gather | solution.py:35
  530.4 35.3 %all-gather.44.cloned.1.call-done = bf16[960,1280]{1,0:T(8,128)(2,1)} async-done(((bf16[480,1280]{1,0:T(8,128)(2,1)}), bf16[960,1280]{1,0:T(8,128)(2,1)}) %all-gather.44.cloned.1.call-update) | async-done | bytes 2457616 | tf_op jit(solution)/shard_map/all_gather | solution.py:35
  565.7 6.9 all_to_all.137
  574.2 30.0 %all-gather.42.cloned.1.call-done = bf16[960,1280]{1,0:T(8,128)(2,1)} async-done(((bf16[480,1280]{1,0:T(8,128)(2,1)}), bf16[960,1280]{1,0:T(8,128)(2,1)}) %all-gather.42.cloned.1.call-update) | async-done | bytes 2457616 | tf_op jit(solution)/shard_map/all_gather | solution.py:35
  604.3 6.9 all_to_all.138
  612.8 32.0 %all-gather.58.cloned.1.call-done = bf16[16,160,480]{2,1,0:T(8,128)(2,1)} async-done(((bf16[8,160,480]{2,1,0:T(8,128)(2,1)}), bf16[16,160,480]{2,1,0:T(8,128)(2,1)}) %all-gather.58.cloned.1.call-update) | async-done | bytes 2457616 | tf_op jit(solution)/shard_map/all_gather | solution.py:149
  644.8 3.5 copy.202
  648.3 20.6 %all-gather.40.cloned.1.call-done = bf16[2048,2560]{1,0:T(8,128)(2,1)} async-done(((bf16[2048,1280]{1,0:T(8,128)(2,1)}), bf16[2048,2560]{1,0:T(8,128)(2,1)}) %all-gather.40.cloned.1.call-update) | async-done | bytes 10485776 | tf_op jit(solution)/shard_map/all_gather | solution.py:35
  668.9 10.2 fusion.158
  679.1 7.2 fusion.157
  686.3 7.9 all-gather.48.cloned.1.call-done
  694.2 16.2 %multiply_reduce_fusion = (f32[480]{0:T(512)}, bf16[2048,480]{0,1:T(8,128)(2,1)}, bf16[2048,480]{0,1:T(8,128)(2,1)}, f32[480]{0:T(512)}, bf16[2048,480]{0,1:T(8,128)(2,1)}) fusion(f32[2048,480]{0,1:T(8,128)} %fusion.157, f32[480]{0:T(512)S(1)} %dynamic_slice.6, f32[2048,480]{0,1:T(8,128)} %fusion.158, f32[480]{0:T(512)S(1)} %dynamic_slice.7, ...), kind=kOutput, calls=%fused_computation.41 | convolution fusion | flops 5062654976 | bytes 26713600 | tf_op jit(solution)/shard_map/dot_general | solution.py:23
  710.3 12.2 fusion.53
  722.6 12.9 add_convert_fusion
  735.5 10.6 convolution_convert_fusion
  746.2 8.5 reduce-scatter.19.cloned.1.call-done
  754.7 21.2 %reduce-scatter.15.cloned.1.call-done = bf16[2048,1280]{1,0:T(8,128)(2,1)} async-done(((bf16[2048,2560]{1,0:T(8,128)(2,1)}), bf16[2048,1280]{1,0:T(8,128)(2,1)}) %reduce-scatter.15.cloned.1.call-update) | async-done | bytes 5242896 | tf_op jit(solution)/shard_map/reduce_scatter | solution.py:39
  776.1 107.7 %reduce-scatter.21.cloned.1.call-done = bf16[256,1280]{1,0:T(8,128)(2,1)} async-done(((bf16[2048,1280]{1,0:T(8,128)(2,1)}), bf16[256,1280]{1,0:T(8,128)(2,1)}) %reduce-scatter.21.cloned.1.call-update) | async-done | bytes 655376 | tf_op jit(solution)/shard_map/reduce_scatter | solution.py:39
  888.3 101.6 %reduce-scatter.17.cloned.1.call-done = bf16[256,1280]{1,0:T(8,128)(2,1)} async-done(((bf16[2048,1280]{1,0:T(8,128)(2,1)}), bf16[256,1280]{1,0:T(8,128)(2,1)}) %reduce-scatter.17.cloned.1.call-update) | async-done | bytes 655376 | tf_op jit(solution)/shard_map/reduce_scatter | solution.py:39
  989.9 3.8 fusion.154
  1001.6 18.2 %all-gather.50.cloned.1.call-done = bf16[512,1280]{1,0:T(8,128)(2,1)} async-done(((bf16[256,1280]{1,0:T(8,128)(2,1)}), bf16[512,1280]{1,0:T(8,128)(2,1)}) %all-gather.50.cloned.1.call-update) | async-done | bytes 1310736 | tf_op jit(solution)/shard_map/all_gather | solution.py:35
  1022.2 6.3 all_to_all.139
  1028.5 7.7 fusion.152
  1036.2 4.6 scan_back.1
  1041.7 21.8 %all-gather.4 = f32[16,2,1280]{2,1,0:T(2,128)S(1)} all-gather(f32[1,2,1280]{2,1,0:T(2,128)S(1)} %maximum_bitcast_fusion.1), channel_id=4, replica_groups=mesh['t'=4,'f'=2,'row'=2,'col'=2] {'t','f','col'}, dimensions={0}, use_global_device_ids=true | all-gather | bytes 174080 | tf_op jit(solution)/shard_map/all_gather | solution.py:90
  1064.1 4.0 fusion.149
  1068.1 3.6 multiply_reduce_fusion.5
  1076.4 6.7 multiply_reduce_fusion.3
  1087.8 9.8 fusion
  1097.6 4.4 copy.216
  1105.5 8.6 convolution_convert_fusion.6
  1114.3 9.4 all_to_all.140
  1123.8 8.6 convolution_convert_fusion.5
  1132.5 6.6 all_to_all.141
  1147.3 6.4 fusion.159
  1154.9 5.5 fusion.7
  1160.6 5.6 all_to_all.142
  1167.6 4.9 convolution_convert_fusion.1
  1173.9 4.9 convolution_convert_fusion.3
  1178.9 5.0 convolution_convert_fusion.2
  1184.0 3.6 all-to-all-start.9
  1190.8 27.2 %reduce-scatter.33.cloned.1.call-done = bf16[480,1280]{1,0:T(8,128)(2,1)} async-done(((bf16[960,1280]{1,0:T(8,128)(2,1)}), bf16[480,1280]{1,0:T(8,128)(2,1)}) %reduce-scatter.33.cloned.1.call-update) | async-done | bytes 1228816 | tf_op jit(solution)/shard_map/reduce_scatter | solution.py:39
  1224.3 4.0 reshape.715
  1228.4 96.4 %all-reduce.9.cloned.1.call-done = (f32[20480]{0:T(1024)}, f32[5,256,256]{2,1,0:T(8,128)}, f32[5,256,256]{2,1,0:T(8,128)}) async-done(((f32[20480]{0:T(1024)}, f32[5,256,256]{2,1,0:T(8,128)}, f32[5,256,256]{2,1,0:T(8,128)}), (f32[20480]{0:T(1024)}, f32[5,256,256]{2,1,0:T(8,128)}, f32[5,256,256]{2,1,0:T(8,128)})) %all-reduce.9.cloned.1.call-update) | async-done | bytes 2703376 | tf_op jit(solution)/shard_map/psum | solution.py:356
  1328.9 21.1 %reduce-scatter.23.cloned.1.call-done = bf16[256,1280]{1,0:T(8,128)(2,1)} async-done(((bf16[512,1280]{1,0:T(8,128)(2,1)}), bf16[256,1280]{1,0:T(8,128)(2,1)}) %reduce-scatter.23.cloned.1.call-update) | async-done | bytes 655376 | tf_op jit(solution)/shard_map/reduce_scatter | solution.py:39
  1354.1 77.4 %psum.60 = f32[4,1280]{1,0:T(4,128)S(1)} all-reduce(f32[4,1280]{1,0:T(4,128)S(1)} %pad_maximum_fusion.3), channel_id=1, replica_groups=mesh['t'=4,'f'=2,'row'=2,'col'=2] {'t','f','row'}, use_global_device_ids=true, to_apply=%region_18.19 | all-reduce | flops 5120 | bytes 40960 | tf_op jit(solution)/shard_map/psum | solution.py:329
  1436.7 73.9 %reduce-scatter.25.cloned.1.call-done = bf16[160,1280]{1,0:T(8,128)(2,1)} async-done(((bf16[1280,1280]{1,0:T(8,128)(2,1)}), bf16[160,1280]{1,0:T(8,128)(2,1)}) %reduce-scatter.25.cloned.1.call-update) | async-done | bytes 409616 | tf_op jit(solution)/shard_map/reduce_scatter | solution.py:39
  1512.5 76.7 %reduce-scatter.27.cloned.1.call-done = bf16[160,1280]{1,0:T(8,128)(2,1)} async-done(((bf16[1280,1280]{1,0:T(8,128)(2,1)}), bf16[160,1280]{1,0:T(8,128)(2,1)}) %reduce-scatter.27.cloned.1.call-update) | async-done | bytes 409616 | tf_op jit(solution)/shard_map/reduce_scatter | solution.py:39
  (331 shorter events, 107.6 us)
Async XLA Ops:
  7.2 5.7 copy-start.47
  7.2 67.2 %all-gather.26.cloned.1.call-start = ((), (), s32[]{:S(2)}) async-start(), calls=%async_computation.23 | async-start | bytes 3686400 | tf_op jit(solution)/shard_map/all_gather | solution.py:35
  7.9 128.8 %all-gather.30.cloned.1.call-start = ((), (), s32[]{:S(2)}) async-start(), calls=%async_computation.25 | async-start | bytes 3686400 | tf_op jit(solution)/shard_map/all_gather | solution.py:35
  8.7 190.4 %all-gather.34.cloned.1.call-start = ((), (), s32[]{:S(2)}) async-start(), calls=%async_computation.27 | async-start | bytes 3686400 | tf_op jit(solution)/shard_map/all_gather | solution.py:35
  9.4 214.6 %all-gather.24.cloned.1.call-start = ((), (), s32[]{:S(2)}) async-start(), calls=%async_computation.22 | async-start | bytes 1966080 | tf_op jit(solution)/shard_map/all_gather | solution.py:35
  12.9 61.6 %copy-start.42 = (f32[256,1]{0,1:T(1,128)}, f32[256,1]{0,1:T(1,128)S(1)}, u32[]{:S(2)}) copy-start(f32[256,1]{0,1:T(1,128)S(1)} %get-tuple-element.123) | copy-start | bytes 3076
  12.9 61.6 %copy-start.31 = (f32[1280]{0:T(1024)}, f32[1280]{0:T(1024)S(1)}, u32[]{:S(2)}) copy-start(f32[1280]{0:T(1024)S(1)} %broadcast_add_fusion.1) | copy-start | bytes 15364
  14.0 228.7 %all-gather.28.cloned.1.call-start = ((), (), s32[]{:S(2)}) async-start(), calls=%async_computation.24 | async-start | bytes 9830400 | tf_op jit(solution)/shard_map/all_gather | solution.py:35
  74.5 214.1 %all-gather.32.cloned.1.call-start = ((), (), s32[]{:S(2)}) async-start(), calls=%async_computation.26 | async-start | bytes 9830400 | tf_op jit(solution)/shard_map/all_gather | solution.py:35
  136.8 159.4 %all-gather.36.cloned.1.call-start = ((), (), s32[]{:S(2)}) async-start(), calls=%async_computation.28 | async-start | bytes 9830400 | tf_op jit(solution)/shard_map/all_gather | solution.py:35
  199.2 128.5 %reduce-scatter.13.cloned.1.call-start = ((), (), s32[]{:S(2)}) async-start(), calls=%async_computation.29 | async-start | bytes 1966080 | tf_op jit(solution)/shard_map/reduce_scatter | solution.py:39
  199.2 51.7 %copy-start.50 = (pred[256]{0:T(512)(128)(4,1)}, pred[256]{0:T(512)(128)(4,1)S(1)}, u32[]{:S(2)}) copy-start(pred[256]{0:T(512)(128)(4,1)S(1)} %get-tuple-element.162) | copy-start | bytes 772
  199.2 51.7 %copy-start.52 = (pred[256]{0:T(512)(128)(4,1)}, pred[256]{0:T(512)(128)(4,1)S(1)}, u32[]{:S(2)}) copy-start(pred[256]{0:T(512)(128)(4,1)S(1)} %get-tuple-element.163) | copy-start | bytes 772
  199.9 51.1 %copy-start.54 = (pred[256]{0:T(512)(128)(4,1)}, pred[256]{0:T(512)(128)(4,1)S(1)}, u32[]{:S(2)}) copy-start(pred[256]{0:T(512)(128)(4,1)S(1)} %get-tuple-element.160) | copy-start | bytes 772
  199.9 51.1 %copy-start.56 = (pred[256]{0:T(512)(128)(4,1)}, pred[256]{0:T(512)(128)(4,1)S(1)}, u32[]{:S(2)}) copy-start(pred[256]{0:T(512)(128)(4,1)S(1)} %get-tuple-element.161) | copy-start | bytes 772
  225.6 17.0 %copy-start.62 = (f32[1280]{0:T(1024)S(1)}, f32[1280]{0:T(1024)}, u32[]{:S(2)}) copy-start(f32[1280]{0:T(1024)} %param.28) | copy-start | bytes 15364
  242.6 8.3 copy-start.44
  247.8 4.6 copy-start.7
  247.9 3.1 collective-permute-start
  257.6 30.9 %copy-start.63 = (f32[1280]{0:T(1024)S(1)}, f32[1280]{0:T(1024)}, u32[]{:S(2)}) copy-start(f32[1280]{0:T(1024)} %param.26) | copy-start | bytes 15364
  296.2 5.0 copy-start.27
  307.0 20.7 %copy-start.30 = (f32[1280]{0:T(1024)S(1)}, f32[1280]{0:T(1024)}, u32[]{:S(2)}) copy-start(f32[1280]{0:T(1024)} %param.37) | copy-start | bytes 15364
  307.0 135.6 %all-gather.38.cloned.1.call-start = ((), (), s32[]{:S(2)}) async-start(), calls=%async_computation.30 | async-start | bytes 5898240 | tf_op jit(solution)/shard_map/all_gather | solution.py:35
  327.7 4.8 copy-start.6
  333.6 195.2 %all-gather.46.cloned.1.call-start = ((), (), s32[]{:S(2)}) async-start(), calls=%async_computation.36 | async-start | bytes 5898240 | tf_op jit(solution)/shard_map/all_gather | solution.py:35
  334.2 231.5 %all-gather.44.cloned.1.call-start = ((), (), s32[]{:S(2)}) async-start(), calls=%async_computation.33 | async-start | bytes 3686400 | tf_op jit(solution)/shard_map/all_gather | solution.py:35
  334.9 269.4 %all-gather.42.cloned.1.call-start = ((), (), s32[]{:S(2)}) async-start(), calls=%async_computation.32 | async-start | bytes 3686400 | tf_op jit(solution)/shard_map/all_gather | solution.py:35
  335.5 309.4 %all-gather.58.cloned.1.call-start = ((), (), s32[]{:S(2)}) async-start(), calls=%async_computation.51 | async-start | bytes 3932160 | tf_op jit(solution)/shard_map/all_gather | solution.py:149
  395.3 273.6 %all-gather.40.cloned.1.call-start = ((), (), s32[]{:S(2)}) async-start(), calls=%async_computation.31 | async-start | bytes 15728640 | tf_op jit(solution)/shard_map/all_gather | solution.py:35
  442.6 251.5 %all-gather.48.cloned.1.call-start = ((), (), s32[]{:S(2)}) async-start(), calls=%async_computation.37 | async-start | bytes 15728640 | tf_op jit(solution)/shard_map/all_gather | solution.py:35
  528.8 225.9 %reduce-scatter.19.cloned.1.call-start = ((), (), s32[]{:S(2)}) async-start(), calls=%async_computation.38 | async-start | bytes 15728640 | tf_op jit(solution)/shard_map/reduce_scatter | solution.py:39
  668.9 10.2 copy-start.16
  668.9 10.2 copy-start.61
  694.2 16.2 %copy-start.17 = (bf16[2,60,8,1280]{3,2,0,1:T(8,128)(2,1)S(1)}, bf16[2,60,8,1280]{3,2,0,1:T(8,128)(2,1)}, u32[]{:S(2)}) copy-start(bf16[2,60,8,1280]{3,2,0,1:T(8,128)(2,1)} %copy.241) | copy-start | bytes 7372804
  710.3 12.2 copy-start.15
  735.5 40.5 %reduce-scatter.15.cloned.1.call-start = ((), (), s32[]{:S(2)}) async-start(), calls=%async_computation.34 | async-start | bytes 15728640 | tf_op jit(solution)/shard_map/reduce_scatter | solution.py:39
  746.2 137.6 %reduce-scatter.21.cloned.1.call-start = ((), (), s32[]{:S(2)}) async-start(), calls=%async_computation.39 | async-start | bytes 5898240 | tf_op jit(solution)/shard_map/reduce_scatter | solution.py:39
  754.7 235.2 %reduce-scatter.17.cloned.1.call-start = ((), (), s32[]{:S(2)}) async-start(), calls=%async_computation.35 | async-start | bytes 5898240 | tf_op jit(solution)/shard_map/reduce_scatter | solution.py:39
  776.0 243.8 %all-gather.50.cloned.1.call-start = ((), (), s32[]{:S(2)}) async-start(), calls=%async_computation.40 | async-start | bytes 1966080 | tf_op jit(solution)/shard_map/all_gather | solution.py:35
  995.8 170.8 %all-gather.56.cloned.1.call-start = ((), (), s32[]{:S(2)}) async-start(), calls=%async_computation.46 | async-start | bytes 1966080 | tf_op jit(solution)/shard_map/all_gather | solution.py:35
  999.1 173.6 %all-gather.52.cloned.1.call-start = ((), (), s32[]{:S(2)}) async-start(), calls=%async_computation.42 | async-start | bytes 1966080 | tf_op jit(solution)/shard_map/all_gather | solution.py:35
  1022.2 6.3 copy-start.25
  1022.2 6.3 copy-start.64
  1036.2 27.8 %copy-start.46 = (pred[256]{0:T(512)(128)(4,1)S(1)}, pred[256]{0:T(512)(128)(4,1)}, u32[]{:S(2)}) copy-start(pred[256]{0:T(512)(128)(4,1)} %copy-done.45) | copy-start | bytes 772
  1076.4 102.5 %all-gather.54.cloned.1.call-start = ((), (), s32[]{:S(2)}) async-start(), calls=%async_computation.44 | async-start | bytes 1966080 | tf_op jit(solution)/shard_map/all_gather | solution.py:35
  1083.7 3.1 collective-permute-start.1
  1087.8 96.2 %reduce-scatter.35.cloned.1.call-start = ((), (), s32[]{:S(2)}) async-start(), calls=%async_computation.50 | async-start | bytes 3932160 | tf_op jit(solution)/shard_map/reduce_scatter | solution.py:39
  1105.5 82.1 %reduce-scatter.31.cloned.1.call-start = ((), (), s32[]{:S(2)}) async-start(), calls=%async_computation.48 | async-start | bytes 3686400 | tf_op jit(solution)/shard_map/reduce_scatter | solution.py:39
  1123.7 94.3 %reduce-scatter.33.cloned.1.call-start = ((), (), s32[]{:S(2)}) async-start(), calls=%async_computation.49 | async-start | bytes 3686400 | tf_op jit(solution)/shard_map/reduce_scatter | solution.py:39
  1139.2 185.5 %all-reduce.9.cloned.1.call-start = ((), (), s32[]{:S(2)}) async-start(), calls=%async_computation.52 | async-start | bytes 5406720 | tf_op jit(solution)/shard_map/psum | solution.py:356
  1142.3 5.0 copy-start.28
  1147.3 6.4 copy-start.39
  1147.3 6.4 copy-start.37
  1147.3 6.4 copy-start.38
  1154.5 195.6 %reduce-scatter.23.cloned.1.call-start = ((), (), s32[]{:S(2)}) async-start(), calls=%async_computation.41 | async-start | bytes 1966080 | tf_op jit(solution)/shard_map/reduce_scatter | solution.py:39
  1166.3 268.5 %reduce-scatter.29.cloned.1.call-start = ((), (), s32[]{:S(2)}) async-start(), calls=%async_computation.47 | async-start | bytes 3686400 | tf_op jit(solution)/shard_map/reduce_scatter | solution.py:39
  1172.6 338.0 %reduce-scatter.25.cloned.1.call-start = ((), (), s32[]{:S(2)}) async-start(), calls=%async_computation.43 | async-start | bytes 3686400 | tf_op jit(solution)/shard_map/reduce_scatter | solution.py:39
  1178.8 410.4 %reduce-scatter.27.cloned.1.call-start = ((), (), s32[]{:S(2)}) async-start(), calls=%async_computation.45 | async-start | bytes 3686400 | tf_op jit(solution)/shard_map/reduce_scatter | solution.py:39
  1184.0 37.0 %all-to-all-start.9 = ((bf16[8,160,480]{2,1,0:T(8,128)(2,1)}), bf16[8,160,480]{2,1,0:T(8,128)(2,1)S(1)}, u32[]{:S(2)}, u32[]{:S(2)}) async-start(bf16[8,160,480]{2,1,0:T(8,128)(2,1)} %bitcast.432), calls=%async_computation.21 | async-start | bytes 2621440 | tf_op jit(solution)/shard_map/all_to_all | solution.py:43
  1224.3 125.8 %copy-start.32 = (f32[1280]{0:T(1024)S(1)}, f32[1280]{0:T(1024)}, u32[]{:S(2)}) copy-start(f32[1280]{0:T(1024)} %copy-done.31) | copy-start | bytes 15364
  1224.3 125.8 %copy-start.43 = (f32[256,1]{0,1:T(1,128)S(1)}, f32[256,1]{0,1:T(1,128)}, u32[]{:S(2)}) copy-start(f32[256,1]{0,1:T(1,128)} %copy-done.42) | copy-start | bytes 3076
  1228.3 203.8 %copy-start.5 = (f32[256,1280]{1,0:T(8,128)S(1)}, f32[256,1280]{1,0:T(8,128)}, u32[]{:S(2)}) copy-start(f32[256,1280]{1,0:T(8,128)} %copy-done.4) | copy-start | bytes 3932164
  1228.3 203.8 %copy-start.58 = (f32[256,1]{0,1:T(1,128)S(1)}, f32[256,1]{0,1:T(1,128)}, u32[]{:S(2)}) copy-start(f32[256,1]{0,1:T(1,128)} %get-tuple-element.122) | copy-start | bytes 3076
  1436.7 154.5 %copy-start.23 = (f32[5,256,256]{2,1,0:T(8,128)S(1)}, f32[5,256,256]{2,1,0:T(8,128)}, u32[]{:S(2)}) copy-start(f32[5,256,256]{2,1,0:T(8,128)} %get-tuple-element.184) | copy-start | bytes 3932164
  (35 other events, 64.1 us)
Sparse Core Ops, SparseCore 0:
  10.2 64.1 all-gather.25
  76.6 60.1 all-gather.29
  139.0 60.1 all-gather.33
  201.1 22.8 all-gather.23
  225.4 17.1 all-gather.27
  244.0 18.3 all-gather.31
  263.9 18.3 all-gather.35
  307.1 20.4 reduce-scatter.12
  333.7 108.8 all-gather.37
  444.6 84.0 all-gather.45
  530.3 35.3 all-gather.43
  567.1 37.1 all-gather.41
  605.8 38.9 all-gather.57
  646.3 22.6 all-gather.39
  670.3 23.7 all-gather.47
  735.6 19.0 reduce-scatter.18
  756.8 19.1 reduce-scatter.14
  779.4 104.2 reduce-scatter.20
  887.3 102.5 reduce-scatter.16
  995.9 23.8 all-gather.49
  1021.3 9.4 all-gather.55
  1076.5 5.9 all-gather.51
  1087.9 7.9 all-gather.53
  1105.6 36.2 reduce-scatter.34
  1144.1 35.8 reduce-scatter.30
  1182.1 35.8 reduce-scatter.32
  1223.0 101.6 all-reduce.8
  1327.0 23.0 reduce-scatter.22
  1353.7 77.6 reduce-scatter.28
  1434.9 75.6 reduce-scatter.24
  1514.2 75.0 reduce-scatter.26
